TPU v7x, 32 devices: a whole 2x2x4 slice. The times are simulated.
32 devices in a mesh: pw: 8 (over y, x, core), mode: 4 (over z).
Axes of the slice: x: 2, y: 2, z: 4, core: 2. Of those that a mesh axis runs over, the one named last changes fastest.
Arguments:
- wave_coeffs: bfloat16 [2, 192, 32768], P(None, 'mode', 'pw'), may hold values from -0.03125 to 0.03125
- sphere_map: int32 [32768], P('pw'), may hold values from 0 to 32768, as said below
- wave_kq: bfloat16 [192, 64, 64, 128], P(None, 'pw'), may hold values from -6 to 6
- potential: bfloat16 [4, 64, 64, 128], P('mode', 'pw'), may hold values from -6 to 6
- shift_map: int32 [3], replicated, may hold values from -1 to 1
Outputs:
- coupling: float32 [192, 2, 192, 4], P('pw', None, None, 'mode')
Inputs may be any that keep to these rules, and one draw needn't show every extreme that they name: `sphere_map`: entries 4096 * p to 4096 * (p + 1) - 1 belong to pw shard p, whose grid planes are g1 = p * 64 / 8 and the next ones. A live entry is a cell of that shard's planes, numbered (local plane * 64 + g2) * 64 + g3, and live entries of one shard are distinct; the value 32768 marks an unused slot. Some shards use all their slots.
All inputs are finite; a program needn't handle non-finite values.
Results may differ from a plain program's by a relative error of at most 0.023.
Values may be sent and summed in bfloat16 or wider, within the bound.
No kernel may reach another device: no remote copies, remote signals or barrier semaphores. Data moves between devices by JAX's collectives and lax.ppermute only.
A program may use at most 256 MiB of HBM per device.

v0:
```python
import math
import jax
import jax.numpy as jnp
from jax import lax
from jax.sharding import PartitionSpec as P

NG = 64


def dft_matrix():
    positions = jnp.arange(NG, dtype=jnp.int32)
    angles = (positions[:, None] * positions[None, :] % NG).astype(jnp.float32) * (
        2.0 * math.pi / NG
    )
    cosine = jnp.cos(angles)
    sine_table = jnp.sin(angles)
    upper = jnp.concatenate([cosine, sine_table], 1)
    lower = jnp.concatenate([-sine_table, cosine], 1)
    return jnp.concatenate([upper, lower], 0).astype(jnp.bfloat16)


def place_cells(coeffs, sphere_map, slab_cells):
    rows = coeffs.shape[0] * coeffs.shape[1]
    flat_coeffs = coeffs.reshape(rows, coeffs.shape[2])
    slot_count = sphere_map.shape[0]
    block = min(1024, slot_count)
    cell_ids = jnp.arange(slab_cells, dtype=jnp.int32)

    def add_block(index, total):
        start = index * block
        targets = lax.dynamic_slice_in_dim(sphere_map, start, block, 0)
        selector = (targets[:, None] == cell_ids[None, :]).astype(jnp.bfloat16)
        values = lax.dynamic_slice_in_dim(flat_coeffs, start, block, 1)
        return total + jnp.dot(values, selector, preferred_element_type=jnp.float32)

    total = lax.fori_loop(
        0, slot_count // block, add_block, jnp.zeros((rows, slab_cells), jnp.float32)
    )
    return total.astype(jnp.bfloat16)


def transform(coeffs, sphere_map, matrix):
    band_count = coeffs.shape[1]
    planes = NG // lax.axis_size("pw")
    slab_cells = planes * NG * NG
    grid_cells = place_cells(coeffs, sphere_map, slab_cells)
    grid_cells = (
        grid_cells.reshape(2, band_count, planes, NG, NG)
        .transpose(1, 2, 3, 0, 4)
        .reshape(band_count, planes, NG, 2 * NG)
    )
    partial_value = jnp.dot(grid_cells, matrix, preferred_element_type=jnp.float32).astype(
        jnp.bfloat16
    )
    partial_value = (
        partial_value.reshape(band_count, planes, NG, 2, NG)
        .transpose(0, 1, 4, 3, 2)
        .reshape(band_count, planes, NG, 2 * NG)
    )
    partial_value = jnp.dot(partial_value, matrix, preferred_element_type=jnp.float32).astype(
        jnp.bfloat16
    )
    partial_value = (
        partial_value.reshape(band_count, planes, NG, 2, NG)
        .transpose(0, 4, 1, 2, 3)
        .reshape(band_count, NG, planes, 2 * NG)
    )
    received = lax.all_to_all(partial_value, "pw", split_axis=1, concat_axis=2, tiled=True)
    row_count = received.shape[0]
    columns = received.shape[1]
    arranged = (
        received.reshape(row_count, columns, NG, NG, 2)
        .transpose(0, 1, 3, 4, 2)
        .reshape(row_count, columns, NG, 2 * NG)
    )
    return jnp.dot(arranged, matrix, preferred_element_type=jnp.float32).astype(jnp.bfloat16)


def on_device(wave_coeffs, sphere_map, wave_kq, potential, shift_map):
    matrix = dft_matrix()
    real_k = transform(wave_coeffs, sphere_map, matrix)
    modes_used = lax.all_gather(potential, "mode", axis=0, tiled=True)
    columns = modes_used.shape[1]
    grid_axis = jnp.arange(NG, dtype=jnp.int32)
    column_ids = lax.axis_index("pw") * columns + jnp.arange(columns, dtype=jnp.int32)
    phase_sum = (
        shift_map[0] * grid_axis[None, None, :]
        + shift_map[1] * column_ids[:, None, None]
        + shift_map[2] * grid_axis[None, :, None]
    ) % NG
    angles = phase_sum.astype(jnp.float32) * (2.0 * math.pi / NG)
    phase_cos = jnp.cos(angles)
    phase_sin = jnp.sin(angles)
    pot_real = modes_used[..., :NG].astype(jnp.float32)
    pot_imag = modes_used[..., NG:].astype(jnp.float32)
    phase_real = pot_real * phase_cos + pot_imag * phase_sin
    phase_imag = pot_imag * phase_cos - pot_real * phase_sin
    k_real = real_k[..., :NG].astype(jnp.float32)
    k_imag = real_k[..., NG:].astype(jnp.float32)
    weight_real = phase_real[:, None] * k_real[None] - phase_imag[:, None] * k_imag[None]
    weight_imag = phase_real[:, None] * k_imag[None] + phase_imag[:, None] * k_real[None]
    modes_here = modes_used.shape[0]
    band_count = real_k.shape[0]
    pair_count = modes_here * band_count
    direct = (
        jnp.concatenate([weight_real, weight_imag], -1).astype(jnp.bfloat16).reshape(pair_count, -1)
    )
    swapped = (
        jnp.concatenate([weight_imag, -weight_real], -1)
        .astype(jnp.bfloat16)
        .reshape(pair_count, -1)
    )
    scale_factor = float(NG) ** (-1.5)
    contract = (((1,), (1,)), ((), ()))
    own_rows = wave_kq.shape[0] // lax.axis_size("pw")
    kq_block = wave_kq.reshape(own_rows * lax.axis_size("pw"), -1)
    g_real = lax.dot_general(kq_block, direct, contract, preferred_element_type=jnp.float32)
    g_imag = lax.dot_general(kq_block, swapped, contract, preferred_element_type=jnp.float32)
    joined = jnp.stack([g_real, g_imag], 1) * scale_factor
    summed = lax.psum_scatter(
        joined.reshape(own_rows * lax.axis_size("pw"), 2, modes_here, band_count)
        .transpose(0, 1, 3, 2)
        .astype(jnp.bfloat16),
        "pw",
        scatter_dimension=0,
        tiled=True,
    ).astype(jnp.float32)
    summed = lax.all_to_all(summed, "mode", split_axis=3, concat_axis=2, tiled=True)
    return summed


def solution(mesh):
    placed = (
        P(None, "mode", "pw"),
        P("pw"),
        P(None, "pw", None, None),
        P("mode", "pw", None, None),
        P(),
    )
    return jax.shard_map(
        on_device,
        mesh=mesh,
        in_specs=placed,
        out_specs=P("pw", None, None, "mode"),
        check_vma=False,
    )
```

profile of v0, /device:TPU:0, one launch (start us, length us, event | category | flops | bytes accessed | tf_op | source)
XLA Modules:
  0.0 780.2 jit_solution(4165691497452577595)
XLA Ops:
  6.5 0.2 negate_convert_fusion.1
  6.7 0.1 fusion.30
  6.8 131.0 %while.14 = (s32[]{:T(128)}, f32[96,32768]{1,0:T(8,128)}, bf16[96,4096]{1,0:T(8,128)(2,1)}, s32[4096]{0:T(1024)}, s32[]{:T(128)}, /*index=5*/s32[]{:T(128)}, s32[]{:T(128)}, s32[]{:T(128)}) while((s32[]{:T(128)}, f32[96,32768]{1,0:T(8,128)}, bf16[96,4096]{1,0:T(8,128)(2,1)}, s32[4096]{0:T(1024)}, s32[]{:T(128)}, ...), condition=%wide.region_1.2_spmd.clone, body=%wide.region_0.1_spmd.clone.sunk | while | flops 6482296832 | bytes 25374868 | solution.py:36
  6.9 0.7 dynamic_slice.21
  7.6 31.3 %fusion.40 = f32[96,32768]{1,0:T(8,128)} fusion(s32[1024]{0:T(1024)S(1)} %dynamic_slice.21, f32[96,32768]{1,0:T(8,128)} %get-tuple-element.175, pred[]{:T(512)S(6)} %compare.10, bf16[96,4096]{1,0:T(8,128)(2,1)} %get-tuple-element.184, s32[]{:T(128)S(6)} %select_n.60), kind=kOutput, calls=%fused_computation.4.clone.1 | convolution fusion | flops 6482296832 | bytes 25366532 | tf_op jit(solution)/shard_map/while/body/eval_jaxpr/dot_general | solution.py:34
  38.9 0.7 dynamic_slice.21
  39.6 32.3 %fusion.40 = f32[96,32768]{1,0:T(8,128)} fusion(s32[1024]{0:T(1024)S(1)} %dynamic_slice.21, f32[96,32768]{1,0:T(8,128)} %get-tuple-element.175, pred[]{:T(512)S(6)} %compare.10, bf16[96,4096]{1,0:T(8,128)(2,1)} %get-tuple-element.184, s32[]{:T(128)S(6)} %select_n.60), kind=kOutput, calls=%fused_computation.4.clone.1 | convolution fusion | flops 6482296832 | bytes 25366532 | tf_op jit(solution)/shard_map/while/body/eval_jaxpr/dot_general | solution.py:34
  71.9 0.7 dynamic_slice.21
  72.6 32.3 %fusion.40 = f32[96,32768]{1,0:T(8,128)} fusion(s32[1024]{0:T(1024)S(1)} %dynamic_slice.21, f32[96,32768]{1,0:T(8,128)} %get-tuple-element.175, pred[]{:T(512)S(6)} %compare.10, bf16[96,4096]{1,0:T(8,128)(2,1)} %get-tuple-element.184, s32[]{:T(128)S(6)} %select_n.60), kind=kOutput, calls=%fused_computation.4.clone.1 | convolution fusion | flops 6482296832 | bytes 25366532 | tf_op jit(solution)/shard_map/while/body/eval_jaxpr/dot_general | solution.py:34
  104.9 0.7 dynamic_slice.21
  105.6 32.3 %fusion.40 = f32[96,32768]{1,0:T(8,128)} fusion(s32[1024]{0:T(1024)S(1)} %dynamic_slice.21, f32[96,32768]{1,0:T(8,128)} %get-tuple-element.175, pred[]{:T(512)S(6)} %compare.10, bf16[96,4096]{1,0:T(8,128)(2,1)} %get-tuple-element.184, s32[]{:T(128)S(6)} %select_n.60), kind=kOutput, calls=%fused_computation.4.clone.1 | convolution fusion | flops 6482296832 | bytes 25366532 | tf_op jit(solution)/shard_map/while/body/eval_jaxpr/dot_general | solution.py:34
  137.9 7.9 %convert_element_type.81 = bf16[96,32768]{1,0:T(8,128)(2,1)} convert(f32[96,32768]{1,0:T(8,128)} %get-tuple-element.99) | non-fusion elementwise | flops 3145728 | bytes 18874368 | tf_op jit(solution)/shard_map/convert_element_type | solution.py:39
  145.8 16.2 %reshape.123 = bf16[2,48,8,64,64]{4,3,2,1,0:T(8,128)(2,1)} reshape(bf16[96,32768]{1,0:T(8,128)(2,1)} %convert_element_type.81) | data formatting | bytes 12582912 | tf_op jit(solution)/shard_map/reshape | solution.py:48
  162.0 23.7 %copy.45 = bf16[48,8,64,2,64]{4,3,2,1,0:T(2,128)(2,1)} copy(bf16[48,8,64,2,64]{4,2,1,0,3:T(8,128)(2,1)} %bitcast.64) | data formatting | bytes 12582912 | tf_op jit(solution)/shard_map/transpose | solution.py:49
  185.7 20.7 %reshape.124 = bf16[48,8,64,128]{3,2,1,0:T(8,128)(2,1)} reshape(bf16[48,8,64,2,64]{4,3,2,1,0:T(2,128)(2,1)} %copy.45) | data formatting | bytes 12582912 | tf_op jit(solution)/shard_map/reshape | solution.py:50
  206.4 7.2 convolution_convert_fusion.2
  213.7 21.6 %reshape.125 = bf16[48,8,64,2,64]{4,3,2,1,0:T(2,128)(2,1)} reshape(bf16[48,8,64,128]{3,2,1,0:T(8,128)(2,1)} %convolution_convert_fusion.2) | data formatting | bytes 12582912 | tf_op jit(solution)/shard_map/reshape | solution.py:56
  235.2 41.2 %copy.46 = bf16[48,8,64,2,64]{4,3,2,1,0:T(2,128)(2,1)} copy(bf16[48,8,64,2,64]{2,3,4,1,0:T(2,128)(2,1)} %bitcast.65) | data formatting | bytes 12582912 | tf_op jit(solution)/shard_map/transpose | solution.py:57
  276.5 20.5 %reshape.126 = bf16[48,8,64,128]{3,2,1,0:T(8,128)(2,1)} reshape(bf16[48,8,64,2,64]{4,3,2,1,0:T(2,128)(2,1)} %copy.46) | data formatting | bytes 12582912 | tf_op jit(solution)/shard_map/reshape | solution.py:58
  297.0 7.2 convolution_convert_fusion.1
  304.2 21.6 %reshape.127 = bf16[48,8,64,2,64]{4,3,2,1,0:T(2,128)(2,1)} reshape(bf16[48,8,64,128]{3,2,1,0:T(8,128)(2,1)} %convolution_convert_fusion.1) | data formatting | bytes 12582912 | tf_op jit(solution)/shard_map/reshape | solution.py:64
  325.8 0.0 copy-start.1
  325.8 0.0 copy-start
  325.8 28.0 %copy.47 = bf16[48,8,64,2,64]{4,1,3,2,0:T(8,128)(2,1)} copy(bf16[48,8,64,2,64]{4,3,2,1,0:T(2,128)(2,1)} %reshape.127) | data formatting | bytes 12582912 | tf_op jit(solution)/shard_map/reshape | solution.py:64
  353.8 17.1 %copy.48 = bf16[48,64,8,128]{3,2,0,1:T(8,128)(2,1)} copy(bf16[48,64,8,128]{1,2,3,0:T(8,128)(2,1)} %bitcast.66) | data formatting | bytes 12582912 | tf_op jit(solution)/shard_map/reshape | solution.py:66
  370.9 5.2 all-to-all-start
  376.1 0.0 all-reduce.3.cloned.1.call-start
  376.2 0.0 copy-done.1
  376.2 0.7 fusion.31
  376.8 0.6 iota_multiply_fusion.1
  377.5 0.6 iota_multiply_fusion
  378.1 0.6 add_multiply_fusion
  378.8 0.0 copy-done
  378.8 17.3 %all_gather.3 = bf16[4,8,64,128]{3,2,1,0:T(8,128)(2,1)S(1)} all-gather(bf16[1,8,64,128]{3,2,1,0:T(8,128)(2,1)S(1)} %copy-done), channel_id=1, replica_groups=mesh['pw'=8,'mode'=4] {'mode'}, dimensions={0}, use_global_device_ids=true | all-gather | bytes 655360 | tf_op jit(solution)/shard_map/all_gather | solution.py:82
  396.1 0.1 broadcast_add_fusion
  396.2 1.1 fusion.22
  397.3 0.4 fusion.14
  397.7 50.2 %all-to-all-done = bf16[48,64,8,128]{3,2,0,1:T(8,128)(2,1)} async-done(((bf16[48,64,8,128]{3,2,0,1:T(8,128)(2,1)}), bf16[48,64,8,128]{3,2,0,1:T(8,128)(2,1)}, u32[]{:S(2)}, u32[]{:S(2)}) %all-to-all-start) | async-done | bytes 6291488 | tf_op jit(solution)/shard_map/all_to_all | solution.py:68
  447.9 29.3 %copy.50 = bf16[48,8,8,8,128]{0,3,2,4,1:T(8,128)(2,1)} copy(bf16[48,8,8,8,128]{4,3,0,1,2:T(8,128)(2,1)} %bitcast.12) | data formatting | bytes 12582912 | tf_op jit(solution)/shard_map/all_to_all | solution.py:68
  477.2 17.4 %copy.60 = bf16[48,8,64,128]{3,2,1,0:T(8,128)(2,1)} copy(bf16[48,8,64,128]{0,3,2,1:T(8,128)(2,1)} %bitcast.63) | data formatting | bytes 12582912 | tf_op jit(solution)/shard_map/reshape | solution.py:74
  494.6 4.6 convolution_convert_fusion
  499.3 9.4 %slice_convert_fusion.1 = (f32[48,8,64,64]{3,2,1,0:T(8,128)}, f32[48,8,64,64]{3,2,1,0:T(8,128)}) fusion(bf16[48,8,64,128]{3,2,1,0:T(8,128)(2,1)S(1)} %convolution_convert_fusion), kind=kLoop, calls=%fused_computation.20 | loop fusion | flops 3145728 | bytes 18874368 | tf_op jit(solution)/shard_map/convert_element_type | solution.py:98
  508.7 32.5 %fusion.7 = (bf16[4,48,8,64,64]{4,3,2,1,0:T(8,128)(2,1)}, bf16[4,48,8,64,64]{4,3,2,1,0:T(8,128)(2,1)}, bf16[4,48,8,64,64]{4,3,2,1,0:T(8,128)(2,1)}) fusion(f32[48,8,64,64]{3,2,1,0:T(8,128)} %get-tuple-element.131, f32[4,8,64,64]{3,2,1,0:T(8,128)S(1)} %get-tuple-element.133, f32[48,8,64,64]{3,2,1,0:T(8,128)} %get-tuple-element.130, ...), kind=kLoop, calls=%fused_computation.10 | loop fusion | flops 62914560 | bytes 51380224 | tf_op jit(solution)/shard_map/convert.2
  541.2 56.0 %pad_maximum_fusion = (bf16[4,48,8,64,128]{4,3,2,1,0:T(8,128)(2,1)}, bf16[4,48,8,64,128]{4,3,2,1,0:T(8,128)(2,1)}) fusion(bf16[4,48,8,64,64]{4,3,2,1,0:T(8,128)(2,1)} %get-tuple-element.126, bf16[4,48,8,64,64]{4,3,2,1,0:T(8,128)(2,1)} %get-tuple-element.125, bf16[4,48,8,64,64]{4,3,2,1,0:T(8,128)(2,1)} %get-tuple-element.127), kind=kLoop, calls=%fused_computation.15 | loop fusion | flops 100663296 | bytes 88080384 | tf_op jit(solution)/shard_map/concatenate | solution.py:106
  597.2 29.8 %convert_element_type.88 = bf16[192,65536]{1,0:T(8,128)(2,1)} reshape(bf16[4,48,8,64,128]{4,3,2,1,0:T(8,128)(2,1)} %get-tuple-element.128) | data formatting | bytes 50331648 | tf_op jit(solution)/shard_map/convert_element_type | solution.py:106
  627.0 23.6 %fusion.10 = f32[192,192]{1,0:T(8,128)S(1)} fusion(bf16[192,65536]{1,0:T(8,128)(2,1)} %convert_element_type.88, bf16[24,8,512,128]{3,2,1,0:T(8,128)(2,1)} %bitcast.69), kind=kOutput, calls=%fused_computation.13 | convolution fusion | flops 4831838208 | bytes 50479104 | tf_op jit(solution)/shard_map/dot_general | solution.py:117
  650.6 0.2 copy.52
  650.8 29.8 %convert_element_type.89 = bf16[192,65536]{1,0:T(8,128)(2,1)} reshape(bf16[4,48,8,64,128]{4,3,2,1,0:T(8,128)(2,1)} %get-tuple-element.129) | data formatting | bytes 50331648 | tf_op jit(solution)/shard_map/convert_element_type | solution.py:110
  680.7 0.0 copy-start.2
  680.7 23.4 %fusion.8 = f32[192,192]{1,0:T(8,128)S(1)} fusion(bf16[192,65536]{1,0:T(8,128)(2,1)} %convert_element_type.89, bf16[24,8,512,128]{3,2,1,0:T(8,128)(2,1)} %bitcast.70), kind=kOutput, calls=%fused_computation.11 | convolution fusion | flops 4831838208 | bytes 50479104 | tf_op jit(solution)/shard_map/dot_general | solution.py:118
  704.1 0.2 copy.53
  704.3 1.0 fusion.17
  705.3 0.0 all-reduce.3.cloned.1.call-update
  705.4 0.0 copy-done.2
  705.4 0.6 dynamic-slice
  706.6 53.4 %all-reduce.3.cloned.1.call-done = bf16[192,2,48,4]{2,3,1,0:T(4,128)(2,1)} async-done(((bf16[192,2,48,4]{2,3,1,0:T(4,128)(2,1)}), bf16[192,2,48,4]{2,3,1,0:T(4,128)(2,1)}) %all-reduce.3.cloned.1.call-update) | async-done | bytes 147472
  760.0 0.8 constant_dynamic-slice_fusion
  760.9 0.1 reshape.135
  761.0 10.0 %all_to_all.33 = f32[4,1,2304]{2,1,0:T(1,128)S(1)} all-to-all(f32[4,1,2304]{2,1,0:T(1,128)S(1)} %reshape.135), channel_id=1, replica_groups=mesh['pw'=8,'mode'=4] {'mode'}, dimensions={0} | all-to-all | bytes 73728 | tf_op jit(solution)/shard_map/all_to_all | solution.py:128
  771.0 0.5 broadcast.132
  771.5 0.7 reduce
  772.3 0.1 reshape.136
  772.4 0.8 reshape.133
  (4 shorter events, 0.1 us)
Async XLA Ops:
  325.8 50.4 %copy-start.1 = (s32[3]{0:T(128)S(1)}, s32[3]{0:T(128)}, u32[]{:S(2)}) copy-start(s32[3]{0:T(128)} %param.11) | copy-start | bytes 40
  325.8 53.0 %copy-start = (bf16[1,8,64,128]{3,2,1,0:T(8,128)(2,1)S(1)}, bf16[1,8,64,128]{3,2,1,0:T(8,128)(2,1)}, u32[]{:S(2)}) copy-start(bf16[1,8,64,128]{3,2,1,0:T(8,128)(2,1)} %param.10) | copy-start | bytes 393220
  370.9 77.0 %all-to-all-start = ((bf16[48,64,8,128]{3,2,0,1:T(8,128)(2,1)}), bf16[48,64,8,128]{3,2,0,1:T(8,128)(2,1)}, u32[]{:S(2)}, u32[]{:S(2)}) async-start(bf16[48,64,8,128]{3,2,0,1:T(8,128)(2,1)} %copy.48), calls=%async_computation | async-start | bytes 12582912 | tf_op jit(solution)/shard_map/all_to_all | solution.py:68
  376.1 383.9 %all-reduce.3.cloned.1.call-start = ((), (), s32[]{:S(2)}) async-start(), calls=%async_computation.2 | async-start | bytes 786432
  680.7 24.7 %copy-start.2 = (u32[32]{0:T(128)S(1)}, u32[32]{0:T(128)}, u32[]{:S(2)}) copy-start(u32[32]{0:T(128)} %constant.70) | copy-start | bytes 388
Sparse Core Ops, SparseCore 0:
  705.5 54.5 all-reduce.2
where the time goes:
time: 794 us; the launch traced here: 780 us
  local copies, waits for them, and re-layouts  324 us (41%)
  matrix products  194 us (24%)
  other arithmetic  111 us (14%)
  waiting for transfers between devices  104 us (13%)
  blocking collectives  27.3 us (3%)
  between operations  14.4 us (2%)
    dot_general x4, matrix products, add_block(): return total + jnp.dot(values, selector, preferred_element_type=jnp.float32)  128 us
    reshape x3, local copies, waits for them, and re-layouts, transform(): partial_value.reshape(band_count, planes, NG, 2, NG)  71.2 us
    concatenate x1, other arithmetic, on_device(): jnp.concatenate([weight_real, weight_imag], -1).astype(jnp.bfloat16)  56 us
    unnamed x2, waiting for transfers between devices  53.4 us
    all_to_all x1, waiting for transfers between devices, transform(): lax.all_to_all(partial_value, 'pw', split_axis=1, concat_axis=2, tiled=True)  50.2 us
    transpose x1, local copies, waits for them, and re-layouts, transform(): partial_value = partial_value.reshape(band_count, planes, NG, 2, NG).tran...  41.2 us
    reshape x2, local copies, waits for them, and re-layouts, transform(): partial_value = partial_value.reshape(band_count, planes, NG, 2, NG).tran...  37.6 us
    another operation x3, other arithmetic  32.8 us
  transfers between devices with their start and end apart: 2, of which 2 were waited for; matrix products, arithmetic and copies ran while one was open for 1% of the time, Pallas kernels for 0%

commit v1 on v0

--- a/solution.py
+++ b/solution.py
@@ -65,7 +65,15 @@
         .transpose(0, 4, 1, 2, 3)
         .reshape(band_count, NG, planes, 2 * NG)
     )
-    received = lax.all_to_all(partial_value, "pw", split_axis=1, concat_axis=2, tiled=True)
+    received = jnp.concatenate(
+        lax.all_to_all(
+            jnp.stack(jnp.split(partial_value, lax.axis_size("pw"), 1), 0),
+            axis_name="pw",
+            split_axis=0,
+            concat_axis=0,
+        ),
+        2,
+    )
     row_count = received.shape[0]
     columns = received.shape[1]
     arranged = (

time: 794 us -> 954 us (1.20)
  local copies, waits for them, and re-layouts: 324 us -> 481 us
    another operation x0 -> x10, local copies, waits for them, and re-layouts: none -> 165 us  [transform(): jnp.stack(jnp.split(partial_value, lax.axis_size('pw'), 1), 0)]
    all_to_all x1 -> x0, local copies, waits for them, and re-layouts: 29.3 us -> none  [transform(): lax.all_to_all(partial_value, 'pw', split_axis=1, concat_axis=2, tiled=True)]
    reshape x0 -> x1, local copies, waits for them, and re-layouts: none -> 28.8 us  [transform(): jnp.concatenate(lax.all_to_all(jnp.stack(jnp.split(partial_value, lax.axi...]
    reshape x2 -> x1, local copies, waits for them, and re-layouts: 37.6 us -> 20.5 us  [transform(): partial_value = partial_value.reshape(band_count, planes, NG, 2, NG).tran...]
    unnamed x10 -> x17, local copies, waits for them, and re-layouts: 1.65 us -> 11.7 us
where the time goes in v1:
time: 954 us; the launch traced here: 938 us
  local copies, waits for them, and re-layouts  481 us (50%)
  matrix products  194 us (20%)
  other arithmetic  112 us (12%)
  waiting for transfers between devices  104 us (11%)
  blocking collectives  27.3 us (3%)
  between operations  14.7 us (2%)
    another operation x10, local copies, waits for them, and re-layouts, transform(): jnp.stack(jnp.split(partial_value, lax.axis_size('pw'), 1), 0)  165 us
    dot_general x4, matrix products, add_block(): return total + jnp.dot(values, selector, preferred_element_type=jnp.float32)  128 us
    reshape x3, local copies, waits for them, and re-layouts, transform(): partial_value.reshape(band_count, planes, NG, 2, NG)  71.3 us
    concatenate x1, other arithmetic, on_device(): jnp.concatenate([weight_real, weight_imag], -1).astype(jnp.bfloat16)  56 us
    unnamed x2, waiting for transfers between devices  53.4 us
    all_to_all x1, waiting for transfers between devices, transform(): lax.all_to_all(jnp.stack(jnp.split(partial_value, lax.axis_size('pw'), 1)...  50.2 us
    transpose x1, local copies, waits for them, and re-layouts, transform(): partial_value = partial_value.reshape(band_count, planes, NG, 2, NG).tran...  41.2 us
    another operation x3, other arithmetic  33.1 us
  transfers between devices with their start and end apart: 2, of which 2 were waited for; matrix products, arithmetic and copies ran while one was open for 1% of the time, Pallas kernels for 0%

profile of v1, /device:TPU:0, one launch (start us, length us, event | category | flops | bytes accessed | tf_op | source)
XLA Modules:
  0.0 938.5 jit_solution(15454655216247000630)
XLA Ops:
  6.8 131.0 %while.14 = (s32[]{:T(128)}, f32[96,32768]{1,0:T(8,128)}, bf16[96,4096]{1,0:T(8,128)(2,1)}, s32[4096]{0:T(1024)}, s32[]{:T(128)}, /*index=5*/s32[]{:T(128)}, s32[]{:T(128)}, s32[]{:T(128)}) while((s32[]{:T(128)}, f32[96,32768]{1,0:T(8,128)}, bf16[96,4096]{1,0:T(8,128)(2,1)}, s32[4096]{0:T(1024)}, s32[]{:T(128)}, ...), condition=%wide.region_1.2_spmd.clone, body=%wide.region_0.1_spmd.clone.sunk | while | flops 6482296832 | bytes 25374868 | solution.py:36
  6.9 0.7 dynamic_slice.21
  7.6 31.3 %fusion.40 = f32[96,32768]{1,0:T(8,128)} fusion(s32[1024]{0:T(1024)S(1)} %dynamic_slice.21, f32[96,32768]{1,0:T(8,128)} %get-tuple-element.183, pred[]{:T(512)S(6)} %compare.10, bf16[96,4096]{1,0:T(8,128)(2,1)} %get-tuple-element.192, s32[]{:T(128)S(6)} %select_n.60), kind=kOutput, calls=%fused_computation.4.clone.1 | convolution fusion | flops 6482296832 | bytes 25366532 | tf_op jit(solution)/shard_map/while/body/eval_jaxpr/dot_general | solution.py:34
  38.9 0.7 dynamic_slice.21
  39.6 32.3 %fusion.40 = f32[96,32768]{1,0:T(8,128)} fusion(s32[1024]{0:T(1024)S(1)} %dynamic_slice.21, f32[96,32768]{1,0:T(8,128)} %get-tuple-element.183, pred[]{:T(512)S(6)} %compare.10, bf16[96,4096]{1,0:T(8,128)(2,1)} %get-tuple-element.192, s32[]{:T(128)S(6)} %select_n.60), kind=kOutput, calls=%fused_computation.4.clone.1 | convolution fusion | flops 6482296832 | bytes 25366532 | tf_op jit(solution)/shard_map/while/body/eval_jaxpr/dot_general | solution.py:34
  71.9 0.7 dynamic_slice.21
  72.6 32.3 %fusion.40 = f32[96,32768]{1,0:T(8,128)} fusion(s32[1024]{0:T(1024)S(1)} %dynamic_slice.21, f32[96,32768]{1,0:T(8,128)} %get-tuple-element.183, pred[]{:T(512)S(6)} %compare.10, bf16[96,4096]{1,0:T(8,128)(2,1)} %get-tuple-element.192, s32[]{:T(128)S(6)} %select_n.60), kind=kOutput, calls=%fused_computation.4.clone.1 | convolution fusion | flops 6482296832 | bytes 25366532 | tf_op jit(solution)/shard_map/while/body/eval_jaxpr/dot_general | solution.py:34
  104.9 0.7 dynamic_slice.21
  105.6 32.3 %fusion.40 = f32[96,32768]{1,0:T(8,128)} fusion(s32[1024]{0:T(1024)S(1)} %dynamic_slice.21, f32[96,32768]{1,0:T(8,128)} %get-tuple-element.183, pred[]{:T(512)S(6)} %compare.10, bf16[96,4096]{1,0:T(8,128)(2,1)} %get-tuple-element.192, s32[]{:T(128)S(6)} %select_n.60), kind=kOutput, calls=%fused_computation.4.clone.1 | convolution fusion | flops 6482296832 | bytes 25366532 | tf_op jit(solution)/shard_map/while/body/eval_jaxpr/dot_general | solution.py:34
  137.9 7.9 convert_element_type.81
  145.7 16.2 %reshape.122 = bf16[2,48,8,64,64]{4,3,2,1,0:T(8,128)(2,1)} reshape(bf16[96,32768]{1,0:T(8,128)(2,1)} %convert_element_type.81) | data formatting | bytes 12582912 | tf_op jit(solution)/shard_map/reshape | solution.py:48
  162.0 23.7 %copy.48 = bf16[48,8,64,2,64]{4,3,2,1,0:T(2,128)(2,1)} copy(bf16[48,8,64,2,64]{4,2,1,0,3:T(8,128)(2,1)} %bitcast.79) | data formatting | bytes 12582912 | tf_op jit(solution)/shard_map/transpose | solution.py:49
  185.7 20.7 %reshape.123 = bf16[48,8,64,128]{3,2,1,0:T(8,128)(2,1)} reshape(bf16[48,8,64,2,64]{4,3,2,1,0:T(2,128)(2,1)} %copy.48) | data formatting | bytes 12582912 | tf_op jit(solution)/shard_map/reshape | solution.py:50
  206.4 7.2 convolution_convert_fusion.2
  213.7 21.6 %reshape.124 = bf16[48,8,64,2,64]{4,3,2,1,0:T(2,128)(2,1)} reshape(bf16[48,8,64,128]{3,2,1,0:T(8,128)(2,1)} %convolution_convert_fusion.2) | data formatting | bytes 12582912 | tf_op jit(solution)/shard_map/reshape | solution.py:56
  235.2 41.2 %copy.49 = bf16[48,8,64,2,64]{4,3,2,1,0:T(2,128)(2,1)} copy(bf16[48,8,64,2,64]{2,3,4,1,0:T(2,128)(2,1)} %bitcast.80) | data formatting | bytes 12582912 | tf_op jit(solution)/shard_map/transpose | solution.py:57
  276.4 20.5 %reshape.125 = bf16[48,8,64,128]{3,2,1,0:T(8,128)(2,1)} reshape(bf16[48,8,64,2,64]{4,3,2,1,0:T(2,128)(2,1)} %copy.49) | data formatting | bytes 12582912 | tf_op jit(solution)/shard_map/reshape | solution.py:58
  296.9 7.2 convolution_convert_fusion.1
  304.2 21.6 %reshape.126 = bf16[48,8,64,2,64]{4,3,2,1,0:T(2,128)(2,1)} reshape(bf16[48,8,64,128]{3,2,1,0:T(8,128)(2,1)} %convolution_convert_fusion.1) | data formatting | bytes 12582912 | tf_op jit(solution)/shard_map/reshape | solution.py:64
  325.7 28.2 %copy.50 = bf16[48,8,64,2,64]{4,1,3,2,0:T(8,128)(2,1)} copy(bf16[48,8,64,2,64]{4,3,2,1,0:T(2,128)(2,1)} %reshape.126) | data formatting | bytes 12582912 | tf_op jit(solution)/shard_map/reshape | solution.py:64
  353.9 70.3 %slice_bitcast_fusion = (bf16[1,48,8,8,128]{2,3,4,1,0:T(8,128)(2,1)}, bf16[1,48,8,8,128]{2,3,4,1,0:T(8,128)(2,1)}, bf16[1,48,8,8,128]{2,3,4,1,0:T(8,128)(2,1)}, ...) fusion(bf16[48,64,8,128]{1,2,3,0:T(8,128)(2,1)} %bitcast.77), kind=kLoop, calls=%fused_computation.19 | loop fusion | bytes 12582912 | tf_op jit(solution)/shard_map/stack | solution.py:70
  424.2 11.6 %copy.51 = bf16[1,48,8,8,128]{4,3,2,1,0:T(8,128)(2,1)S(1)} copy(bf16[1,48,8,8,128]{2,3,4,1,0:T(8,128)(2,1)} %get-tuple-element.137) | data formatting | bytes 1572864 | tf_op jit(solution)/shard_map/stack | solution.py:70
  435.8 0.9 constant_dynamic-update-slice_fusion.7
  436.7 12.0 %copy.52 = bf16[1,48,8,8,128]{4,3,2,1,0:T(8,128)(2,1)} copy(bf16[1,48,8,8,128]{2,3,4,1,0:T(8,128)(2,1)} %get-tuple-element.136) | data formatting | bytes 1572864 | tf_op jit(solution)/shard_map/stack | solution.py:70
  448.7 12.0 %copy.53 = bf16[1,48,8,8,128]{4,3,2,1,0:T(8,128)(2,1)} copy(bf16[1,48,8,8,128]{2,3,4,1,0:T(8,128)(2,1)} %get-tuple-element.135) | data formatting | bytes 1572864 | tf_op jit(solution)/shard_map/stack | solution.py:70
  460.7 12.0 %copy.54 = bf16[1,48,8,8,128]{4,3,2,1,0:T(8,128)(2,1)} copy(bf16[1,48,8,8,128]{2,3,4,1,0:T(8,128)(2,1)} %get-tuple-element.134) | data formatting | bytes 1572864 | tf_op jit(solution)/shard_map/stack | solution.py:70
  472.7 11.5 %copy.55 = bf16[1,48,8,8,128]{4,3,2,1,0:T(8,128)(2,1)S(1)} copy(bf16[1,48,8,8,128]{2,3,4,1,0:T(8,128)(2,1)} %get-tuple-element.133) | data formatting | bytes 1572864 | tf_op jit(solution)/shard_map/stack | solution.py:70
  484.2 11.7 %copy.56 = bf16[1,48,8,8,128]{4,3,2,1,0:T(8,128)(2,1)S(1)} copy(bf16[1,48,8,8,128]{2,3,4,1,0:T(8,128)(2,1)} %get-tuple-element.132) | data formatting | bytes 1572864 | tf_op jit(solution)/shard_map/stack | solution.py:70
  496.0 11.6 %copy.57 = bf16[1,48,8,8,128]{4,3,2,1,0:T(8,128)(2,1)S(1)} copy(bf16[1,48,8,8,128]{2,3,4,1,0:T(8,128)(2,1)} %get-tuple-element.131) | data formatting | bytes 1572864 | tf_op jit(solution)/shard_map/stack | solution.py:70
  507.5 11.6 %copy.58 = bf16[1,48,8,8,128]{4,3,2,1,0:T(8,128)(2,1)S(1)} copy(bf16[1,48,8,8,128]{2,3,4,1,0:T(8,128)(2,1)} %get-tuple-element.130) | data formatting | bytes 1572864 | tf_op jit(solution)/shard_map/stack | solution.py:70
  519.1 2.1 constant_dynamic-update-slice_fusion.6
  521.3 2.0 constant_dynamic-update-slice_fusion.5
  523.3 2.1 constant_dynamic-update-slice_fusion.4
  525.4 0.9 constant_dynamic-update-slice_fusion.3
  526.3 1.0 constant_dynamic-update-slice_fusion.2
  527.3 1.0 constant_dynamic-update-slice_fusion.1
  528.3 0.9 constant_dynamic-update-slice_fusion
  529.2 5.2 all-to-all-start
  534.4 0.6 fusion.31
  535.1 0.6 iota_multiply_fusion.1
  535.7 0.6 iota_multiply_fusion
  536.4 0.6 add_multiply_fusion
  537.0 17.3 %all_gather.3 = bf16[4,8,64,128]{3,2,1,0:T(8,128)(2,1)S(1)} all-gather(bf16[1,8,64,128]{3,2,1,0:T(8,128)(2,1)S(1)} %copy-done), channel_id=1, replica_groups=mesh['pw'=8,'mode'=4] {'mode'}, dimensions={0}, use_global_device_ids=true | all-gather | bytes 655360 | tf_op jit(solution)/shard_map/all_gather | solution.py:90
  554.4 1.1 fusion.22
  555.5 0.4 fusion.14
  556.0 50.2 %all-to-all-done = bf16[8,48,8,8,128]{4,3,2,1,0:T(8,128)(2,1)} async-done(((bf16[8,48,8,8,128]{4,3,2,1,0:T(8,128)(2,1)}), bf16[8,48,8,8,128]{4,3,2,1,0:T(8,128)(2,1)}, u32[]{:S(2)}, u32[]{:S(2)}) %all-to-all-start) | async-done | bytes 6291488 | tf_op jit(solution)/shard_map/all_to_all | solution.py:69
  606.2 28.8 %copy.59 = bf16[48,8,8,8,128]{0,3,2,4,1:T(8,128)(2,1)} copy(bf16[48,8,8,8,128]{4,3,1,0,2:T(8,128)(2,1)} %bitcast.19) | data formatting | bytes 12582912 | tf_op jit(solution)/shard_map/reshape | solution.py:68
  635.0 17.3 %copy.68 = bf16[48,8,64,128]{3,2,1,0:T(8,128)(2,1)} copy(bf16[48,8,64,128]{0,3,2,1:T(8,128)(2,1)} %bitcast.78) | data formatting | bytes 12582912 | tf_op jit(solution)/shard_map/reshape | solution.py:82
  652.3 4.6 convolution_convert_fusion
  657.0 9.4 %slice_convert_fusion.1 = (f32[48,8,64,64]{3,2,1,0:T(8,128)}, f32[48,8,64,64]{3,2,1,0:T(8,128)}) fusion(bf16[48,8,64,128]{3,2,1,0:T(8,128)(2,1)S(1)} %convolution_convert_fusion), kind=kLoop, calls=%fused_computation.28 | loop fusion | flops 3145728 | bytes 18874368 | tf_op jit(solution)/shard_map/convert_element_type | solution.py:106
  666.4 32.8 %fusion.7 = (bf16[4,48,8,64,64]{4,3,2,1,0:T(8,128)(2,1)}, bf16[4,48,8,64,64]{4,3,2,1,0:T(8,128)(2,1)}, bf16[4,48,8,64,64]{4,3,2,1,0:T(8,128)(2,1)}) fusion(f32[48,8,64,64]{3,2,1,0:T(8,128)} %get-tuple-element.139, f32[4,8,64,64]{3,2,1,0:T(8,128)S(1)} %get-tuple-element.141, f32[48,8,64,64]{3,2,1,0:T(8,128)} %get-tuple-element.138, ...), kind=kLoop, calls=%fused_computation.10 | loop fusion | flops 62914560 | bytes 51380224 | tf_op jit(solution)/shard_map/convert.2
  699.1 56.0 %pad_maximum_fusion = (bf16[4,48,8,64,128]{4,3,2,1,0:T(8,128)(2,1)}, bf16[4,48,8,64,128]{4,3,2,1,0:T(8,128)(2,1)}) fusion(bf16[4,48,8,64,64]{4,3,2,1,0:T(8,128)(2,1)} %get-tuple-element.126, bf16[4,48,8,64,64]{4,3,2,1,0:T(8,128)(2,1)} %get-tuple-element.125, bf16[4,48,8,64,64]{4,3,2,1,0:T(8,128)(2,1)} %get-tuple-element.127), kind=kLoop, calls=%fused_computation.15 | loop fusion | flops 100663296 | bytes 88080384 | tf_op jit(solution)/shard_map/concatenate | solution.py:114
  755.2 29.8 %convert_element_type.88 = bf16[192,65536]{1,0:T(8,128)(2,1)} reshape(bf16[4,48,8,64,128]{4,3,2,1,0:T(8,128)(2,1)} %get-tuple-element.128) | data formatting | bytes 50331648 | tf_op jit(solution)/shard_map/convert_element_type | solution.py:114
  785.0 23.6 %fusion.10 = f32[192,192]{1,0:T(8,128)S(1)} fusion(bf16[192,65536]{1,0:T(8,128)(2,1)} %convert_element_type.88, bf16[24,8,512,128]{3,2,1,0:T(8,128)(2,1)} %bitcast.83), kind=kOutput, calls=%fused_computation.13 | convolution fusion | flops 4831838208 | bytes 50479104 | tf_op jit(solution)/shard_map/dot_general | solution.py:125
  808.8 29.8 %convert_element_type.89 = bf16[192,65536]{1,0:T(8,128)(2,1)} reshape(bf16[4,48,8,64,128]{4,3,2,1,0:T(8,128)(2,1)} %get-tuple-element.129) | data formatting | bytes 50331648 | tf_op jit(solution)/shard_map/convert_element_type | solution.py:118
  838.7 23.4 %fusion.8 = f32[192,192]{1,0:T(8,128)S(1)} fusion(bf16[192,65536]{1,0:T(8,128)(2,1)} %convert_element_type.89, bf16[24,8,512,128]{3,2,1,0:T(8,128)(2,1)} %bitcast.84), kind=kOutput, calls=%fused_computation.11 | convolution fusion | flops 4831838208 | bytes 50479104 | tf_op jit(solution)/shard_map/dot_general | solution.py:126
  862.3 1.0 fusion.17
  863.4 0.6 dynamic-slice
  864.6 53.4 %all-reduce.3.cloned.1.call-done = bf16[192,2,48,4]{2,3,1,0:T(4,128)(2,1)} async-done(((bf16[192,2,48,4]{2,3,1,0:T(4,128)(2,1)}), bf16[192,2,48,4]{2,3,1,0:T(4,128)(2,1)}) %all-reduce.3.cloned.1.call-update) | async-done | bytes 147472
  918.0 0.8 constant_dynamic-slice_fusion
  919.0 10.0 %all_to_all.23 = f32[4,1,2304]{2,1,0:T(1,128)S(1)} all-to-all(f32[4,1,2304]{2,1,0:T(1,128)S(1)} %reshape.134), channel_id=1, replica_groups=mesh['pw'=8,'mode'=4] {'mode'}, dimensions={0} | all-to-all | bytes 73728 | tf_op jit(solution)/shard_map/all_to_all | solution.py:136
  929.0 0.5 broadcast.132
  929.5 0.7 reduce
  930.5 0.8 reshape.132
  (19 shorter events, 1.2 us)
Async XLA Ops:
  519.1 15.3 %copy-start.1 = (s32[3]{0:T(128)S(1)}, s32[3]{0:T(128)}, u32[]{:S(2)}) copy-start(s32[3]{0:T(128)} %param.11) | copy-start | bytes 40
  519.1 17.9 %copy-start = (bf16[1,8,64,128]{3,2,1,0:T(8,128)(2,1)S(1)}, bf16[1,8,64,128]{3,2,1,0:T(8,128)(2,1)}, u32[]{:S(2)}) copy-start(bf16[1,8,64,128]{3,2,1,0:T(8,128)(2,1)} %param.10) | copy-start | bytes 393220
  529.2 77.0 %all-to-all-start = ((bf16[8,48,8,8,128]{4,3,2,1,0:T(8,128)(2,1)}), bf16[8,48,8,8,128]{4,3,2,1,0:T(8,128)(2,1)}, u32[]{:S(2)}, u32[]{:S(2)}) async-start(bf16[8,48,8,8,128]{4,3,2,1,0:T(8,128)(2,1)} %constant_dynamic-update-slice_fusion), calls=%async_computation | async-start | bytes 12582912 | tf_op jit(solution)/shard_map/all_to_all | solution.py:69
  534.4 383.7 %all-reduce.3.cloned.1.call-start = ((), (), s32[]{:S(2)}) async-start(), calls=%async_computation.2 | async-start | bytes 786432
  838.7 24.7 %copy-start.2 = (u32[32]{0:T(128)S(1)}, u32[32]{0:T(128)}, u32[]{:S(2)}) copy-start(u32[32]{0:T(128)} %constant.70) | copy-start | bytes 388
Sparse Core Ops, SparseCore 0:
  863.5 54.5 all-reduce.2
